TPU v7x, 256 devices: a 2x2x32 block of a 4x8x32 slice. The times are simulated.
256 devices in a mesh: groups: 4 (over y, x), expert: 64 (over z, core).
Axes of the slice: x: 2, y: 2, z: 32, core: 2. Of those that a mesh axis runs over, the one named last changes fastest.
The devices are a block of a 4x8x32 slice.
Arguments:
- tokens: bfloat16 [32768, 4096], P(('groups', 'expert')), parts along dimension 0, may hold values from -6 to 6
- router_weight: bfloat16 [4096, 128], replicated, may hold values from -0.078125 to 0.078125
- expert_ids: int32 [32768, 8], P(('groups', 'expert')), parts along dimension 0, may hold values from 0 to 127, all different within a row; in each aligned block of 128 rows (0 to 127, 128 to 255, ...) at most 9 rows name the same one
Outputs:
- expert_rows: bfloat16 [128, 2304, 4096], P('expert', 'groups'), parts along dimension 1
- balance_loss: float32 [4], P('groups'), parts along dimension 0
There are 4 independent parts, one for each index of `groups`. A program takes and returns all parts, laid end to end along the dimension named above; an argument that names none is the same for every part. Nothing has to cross between parts.
Inputs may be any that keep to these rules, and one draw needn't show every extreme that they name: `expert_ids`: each row names 8 different experts; among the rows of one device no expert is named more than 9 times, a bound that some block reaches.
All inputs are finite; a program needn't handle non-finite values.
Results may differ from a plain program's by a relative error of at most 0.0012.
Values may be sent and summed in bfloat16 or wider, within the bound.
A program may use at most 128 MiB of HBM per device.

v0:
```python
import functools

import jax
import jax.numpy as jnp
from jax import lax
from jax.sharding import Mesh
from jax.sharding import PartitionSpec as P

EXPERTS = 128
TOP_K = 8
CAP = 9
EXPERT = ("expert_0", "expert_1")
GROUPS_EXPERT = ("groups", "expert_0", "expert_1")


def in_blocks(shard, dim, peers):
    lengths = shard.shape
    pieces = shard.reshape(*lengths[:dim], peers, lengths[dim] // peers, *lengths[dim + 1 :])
    return jnp.moveaxis(pieces, dim, 0)


def cut_rows(length, count):
    unit = 8 if length >= 8 * count else 1
    return [length // unit * k // count * unit for k in range(1, count)]


def in_order(pieces, dim):
    pieces = jnp.moveaxis(pieces, 0, dim)
    lengths = pieces.shape
    return pieces.reshape(*lengths[:dim], lengths[dim] * lengths[dim + 1], *lengths[dim + 2 :])


def exchange_in_pieces(shard, axis, pieces, split_dim, concat_dim):
    blocks = in_blocks(shard, split_dim, lax.axis_size(axis))
    split_at = max(range(1, max(2, blocks.ndim - 1)), key=lambda d: blocks.shape[d])
    outs = []
    for section in jnp.split(blocks, cut_rows(blocks.shape[split_at], pieces), axis=split_at):
        if section.size:
            outs.append(lax.all_to_all(section, axis, split_axis=0, concat_axis=0, tiled=True))
    return in_order(jnp.concatenate(outs, axis=split_at), concat_dim)


def one_axis_at_a_time(shard, axes):
    return functools.reduce(lax.psum, axes, shard)


def on_device(tokens, router_weight, expert_ids):
    local_rows = tokens.shape[0]
    row_width = tokens.shape[1]
    logits = jnp.dot(tokens, router_weight, preferred_element_type=jnp.float32)
    probability = jax.nn.softmax(logits, axis=-1)
    gates = jax.nn.softmax(jnp.take_along_axis(logits, expert_ids, axis=1), axis=1)
    onehot = jnp.sum(
        (expert_ids[:, :, None] == jnp.arange(EXPERTS, dtype=jnp.int32)[None, None, :]).astype(
            jnp.int32
        ),
        axis=1,
    )
    before = jnp.cumsum(onehot, axis=0) - onehot
    slot_rank = jnp.take_along_axis(before, expert_ids, axis=1)
    slot_index = (expert_ids * CAP + slot_rank).reshape(-1)
    token_index = jnp.repeat(jnp.arange(local_rows, dtype=jnp.int32), TOP_K)
    slot_token = jnp.zeros((EXPERTS * CAP,), jnp.int32).at[slot_index].set(token_index)
    slot_gate = jnp.zeros((EXPERTS * CAP,), jnp.float32).at[slot_index].set(gates.reshape(-1))
    picked = tokens[slot_token]
    outgoing = (slot_gate[:, None] * picked.astype(jnp.float32)).astype(jnp.bfloat16)
    outgoing = outgoing.reshape(EXPERTS, CAP, row_width)
    expert_rows = exchange_in_pieces(outgoing, EXPERT, 2, 0, 1)
    expert_load = jnp.sum(onehot, axis=0).astype(jnp.float32)
    expert_mass = jnp.sum(probability, axis=0)
    token_total = jnp.float32(local_rows * lax.axis_size(EXPERT))
    load_all, mass_all = (
        one_axis_at_a_time(expert_load, EXPERT),
        one_axis_at_a_time(expert_mass, EXPERT),
    )
    summed = jnp.sum(load_all * mass_all)
    balance_loss = EXPERTS * summed / (token_total * token_total * TOP_K)
    return (expert_rows, balance_loss.reshape(1))


def solution(mesh):
    finer = Mesh(
        mesh.devices.reshape(mesh.shape["groups"], 32, 2), ("groups", "expert_0", "expert_1")
    )
    in_specs = (P(GROUPS_EXPERT, None), P(), P(GROUPS_EXPERT, None))
    out_specs = (P(EXPERT, "groups", None), P("groups"))
    return jax.shard_map(
        on_device, mesh=finer, in_specs=in_specs, out_specs=out_specs, check_vma=False
    )
```

profile of v0, /device:TPU:37, one launch (start us, length us, event | category | flops | bytes accessed | tf_op | source)
XLA Modules:
  0.0 1056.4 jit_solution(5879255299308648395)
XLA Ops:
  0.6 0.8 bitcast_or_fusion
  1.4 0.8 copy.39
  2.4 0.2 convert_reduce_fusion
  2.9 6.8 gather_fusion.1
  9.9 0.6 fusion.8
  10.5 7.0 gather_fusion.2
  18.2 4.3 scatter_custom_fusion.1
  22.5 4.3 scatter_custom_fusion
  26.9 0.2 mul.22
  27.1 7.9 gather_fusion
  35.0 17.5 %reshape.85 = f32[64,2,9,4096]{3,2,1,0:T(8,128)} reshape(bf16[1152,4096]{1,0:T(8,128)(2,1)} %gather_fusion) | data formatting | bytes 28311552 | tf_op jit(solution)/shard_map/convert_element_type | solution.py:66
  52.5 18.0 %multiply_convert_fusion = bf16[64,2,9,4096]{3,2,1,0:T(8,128)(2,1)} fusion(f32[64,2,9,4096]{3,2,1,0:T(8,128)} %reshape.85, f32[64,2,9]{2,1,0:T(2,128)S(1)} %mul.22), kind=kLoop, calls=%fused_computation.5 | loop fusion | flops 9437184 | bytes 28316160 | tf_op jit(solution)/shard_map/convert_element_type | solution.py:66
  70.4 7.7 split.8
  78.1 34.4 %all-to-all-start = ((bf16[64,2,4,4096]{3,2,1,0:T(4,128)(2,1)}), bf16[64,2,4,4096]{3,2,1,0:T(4,128)(2,1)}, u32[]{:S(2)}, u32[]{:S(2)}) async-start(bf16[64,2,4,4096]{3,2,1,0:T(4,128)(2,1)} %split.8), calls=%async_computation | async-start | bytes 8388608 | tf_op jit(solution)/shard_map/all_to_all | solution.py:39
  112.5 7.3 split.9
  119.8 12.7 %copy.45 = bf16[64,2,5,4096]{3,1,2,0:T(2,128)(2,1)} copy(bf16[64,2,5,4096]{3,2,1,0:T(8,128)(2,1)S(1)} %split.9) | data formatting | bytes 10485760 | tf_op jit(solution)/shard_map/split | solution.py:37
  132.5 349.0 %all-to-all-done = bf16[64,2,4,4096]{3,2,1,0:T(4,128)(2,1)} async-done(((bf16[64,2,4,4096]{3,2,1,0:T(4,128)(2,1)}), bf16[64,2,4,4096]{3,2,1,0:T(4,128)(2,1)}, u32[]{:S(2)}, u32[]{:S(2)}) %all-to-all-start) | async-done | bytes 4194336 | tf_op jit(solution)/shard_map/all_to_all | solution.py:39
  481.5 17.1 %all-to-all-start.1 = ((bf16[64,2,5,4096]{3,1,2,0:T(2,128)(2,1)}), bf16[64,2,5,4096]{3,1,2,0:T(2,128)(2,1)}, u32[]{:S(2)}, u32[]{:S(2)}) async-start(bf16[64,2,5,4096]{3,1,2,0:T(2,128)(2,1)} %copy.45), calls=%async_computation.1 | async-start | bytes 10485760 | tf_op jit(solution)/shard_map/all_to_all | solution.py:39
  498.7 488.8 %all-reduce = (f32[128]{0:T(128)S(1)}, f32[128]{0:T(128)S(1)}) all-reduce(f32[128]{0:T(128)S(1)} %convert_element_type.21, f32[128]{0:T(128)S(1)} %divide_reduce_fusion), channel_id=1, replica_groups=mesh['groups'=4,'expert_0'=32,'expert_1'=2] {'expert_0'}, use_global_device_ids=true, to_apply=%region_7.8 | all-reduce | flops 256 | bytes 2048 | tf_op jit(solution)/shard_map/psum | solution.py:44
  987.5 17.8 %all-reduce.1 = (f32[128]{0:T(128)S(1)}, f32[128]{0:T(128)S(1)}) all-reduce(f32[128]{0:T(128)S(1)} %get-tuple-element.12, f32[128]{0:T(128)S(1)} %get-tuple-element.13), channel_id=1, replica_groups=mesh['groups'=4,'expert_0'=32,'expert_1'=2] {'expert_1'}, use_global_device_ids=true, to_apply=%region_8.9 | all-reduce | flops 256 | bytes 2048 | tf_op jit(solution)/shard_map/psum | solution.py:44
  1005.3 0.6 multiply_reduce_fusion
  1006.5 8.5 copy.46
  1015.1 25.9 %pad_maximum_fusion = bf16[64,2,9,4096]{3,1,2,0:T(2,128)(2,1)} fusion(bf16[64,2,5,4096]{3,1,2,0:T(2,128)(2,1)} %all-to-all-done.1, bf16[64,2,4,4096]{3,1,2,0:T(2,128)(2,1)} %copy.46), kind=kLoop, calls=%fused_computation.6 | loop fusion | flops 4718592 | bytes 18874368 | tf_op jit(solution)/shard_map/concatenate | solution.py:40
  1040.9 14.3 %copy.47 = bf16[2,576,4096]{2,1,0:T(8,128)(2,1)} copy(bf16[2,576,4096]{2,0,1:T(2,128)(2,1)} %bitcast.13) | data formatting | bytes 18874368
  (33 shorter events, 1.4 us)
Async XLA Ops:
  0.6 9.3 copy-start
  2.8 7.1 copy-start.2
  10.5 7.2 copy-start.3
  78.1 403.4 %all-to-all-start = ((bf16[64,2,4,4096]{3,2,1,0:T(4,128)(2,1)}), bf16[64,2,4,4096]{3,2,1,0:T(4,128)(2,1)}, u32[]{:S(2)}, u32[]{:S(2)}) async-start(bf16[64,2,4,4096]{3,2,1,0:T(4,128)(2,1)} %split.8), calls=%async_computation | async-start | bytes 8388608 | tf_op jit(solution)/shard_map/all_to_all | solution.py:39
  481.5 533.6 %all-to-all-start.1 = ((bf16[64,2,5,4096]{3,1,2,0:T(2,128)(2,1)}), bf16[64,2,5,4096]{3,1,2,0:T(2,128)(2,1)}, u32[]{:S(2)}, u32[]{:S(2)}) async-start(bf16[64,2,5,4096]{3,1,2,0:T(2,128)(2,1)} %copy.45), calls=%async_computation.1 | async-start | bytes 10485760 | tf_op jit(solution)/shard_map/all_to_all | solution.py:39
  1040.9 14.3 %copy-start.1 = (bf16[128,4096]{1,0:T(8,128)(2,1)S(1)}, bf16[128,4096]{1,0:T(8,128)(2,1)}, u32[]{:S(2)}) copy-start(bf16[128,4096]{1,0:T(8,128)(2,1)} %param.3) | copy-start | bytes 3145732
where the time goes:
time: 1060 us
  blocking collectives  507 us (48%)
  waiting for transfers between devices  349 us (33%)
  local copies, waits for them, and re-layouts  100 us (9%)
  starting transfers between devices  51.4 us (5%)
  other arithmetic  45.9 us (4%)
    psum x2, blocking collectives, one_axis_at_a_time(): return functools.reduce(lax.psum, axes, shard)  507 us
    all_to_all x2, waiting for transfers between devices, exchange_in_pieces(): lax.all_to_all(section, axis, split_axis=0, concat_axis=0, tiled=True)  349 us
    all_to_all x2, starting transfers between devices, exchange_in_pieces(): lax.all_to_all(section, axis, split_axis=0, concat_axis=0, tiled=True)  51.4 us
    split x3, local copies, waits for them, and re-layouts, exchange_in_pieces(): jnp.split(blocks, cut_rows(blocks.shape[split_at], pieces), axis=split_at)  27.7 us
    concatenate x1, other arithmetic, exchange_in_pieces(): return in_order(jnp.concatenate(outs, axis=split_at), concat_dim)  25.9 us
  transfers between devices with their start and end apart: 2, of which 1 were waited for; matrix products, arithmetic and copies ran while one was open for 3% of the time, Pallas kernels for 0%

commit v1 on v0

v1 whole, which is shorter than its diff:
```python
import jax
import jax.numpy as jnp
from jax import lax
from jax.experimental import pallas as pl
from jax.experimental.pallas import tpu as pltpu
from jax.sharding import PartitionSpec as P

CAP = 9
LOCAL = 2
CORES = 2
CHIP_SLOTS = CORES * LOCAL * CAP
WINDOW = 32
PIECES = 4
META = PIECES
TAIL = (0, 48, 80, 112)
COLS = 512
F32 = jnp.float32
MESH = pl.DeviceIdType.MESH


def kernel(
    ids_ref, tokens_hbm, weight_hbm,
    out_hbm, loss_ref,
    blocks, tail_long, tail_short, other, metas, other_meta, weight, rows_out, sums, other_sums,
    local_sem, piece_send, piece_recv, pass_send, pass_recv, free_sem, sum_sems,
):
    me = lax.axis_index("expert")
    chips = lax.axis_size("expert") // CORES
    tok = blocks.shape[1]
    width = blocks.shape[2]
    experts = weight.shape[1]
    part = tok // PIECES
    z = me // CORES
    core = me % CORES
    sign = 1 - 2 * core
    far_long = chips // 2
    far_short = chips - 1 - far_long
    sibling = CORES * z + 1 - core
    dirs = (sign, -sign)
    fars = (far_long, far_short)

    def chip_at(distance):
        return lax.rem(z + distance + 2 * chips, chips)

    def to(d):
        return {"expert": CORES * chip_at(dirs[d]) + core}

    def source(d, s):
        return chip_at(-dirs[d] * s)

    load_tokens = pltpu.make_async_copy(tokens_hbm, blocks.at[z], local_sem.at[0])
    load_weight = pltpu.make_async_copy(weight_hbm, weight, local_sem.at[1])
    load_tokens.start()
    load_weight.start()
    barrier = pltpu.get_barrier_semaphore()
    for peer in (to(0), to(1), {"expert": sibling}):
        pl.semaphore_signal(barrier, inc=1, device_id=peer, device_id_type=MESH)
    pl.semaphore_wait(barrier, 3)

    def piece(d, s, k, src, dst):
        return pltpu.make_async_remote_copy(
            src_ref=src, dst_ref=dst,
            send_sem=piece_send.at[d, lax.rem(s, 2), k],
            recv_sem=piece_recv.at[d, s - 1, k],
            device_id=to(d), device_id_type=MESH,
        )

    def full(d, s, k):
        c = source(d, s - 1)
        ref = metas.at[c] if k == META else blocks.at[c, pl.ds(k * part, part)]
        return piece(d, s, k, ref, ref)

    def tail(d, s, k, ref=None):
        c = source(d, s - 1)
        rows = pl.ds(TAIL[k], TAIL[k + 1] - TAIL[k])
        dst = blocks.at[c, rows]
        return piece(d, s, k, dst if ref is None else ref.at[rows], dst)

    def passed(d, c, rows):
        return (
            pltpu.make_async_remote_copy(
                src_ref=blocks.at[c, pl.ds(0, rows)], dst_ref=other.at[d, pl.ds(0, rows)],
                send_sem=pass_send.at[d, 0], recv_sem=pass_recv.at[d, 0],
                device_id={"expert": sibling}, device_id_type=MESH,
            ),
            pltpu.make_async_remote_copy(
                src_ref=metas.at[c], dst_ref=other_meta.at[d],
                send_sem=pass_send.at[d, 1], recv_sem=pass_recv.at[d, 1],
                device_id={"expert": sibling}, device_id_type=MESH,
            ),
        )

    def pass_on(d, c, rows, first):
        if not first:
            pl.semaphore_wait(free_sem.at[d], 1)
        for copy in passed(d, c, rows):
            copy.start()

    def take_pass(d, c, rows):
        for copy in passed(d, c, rows):
            copy.wait_recv()

    def end_pass(d, c, rows, last):
        for copy in passed(d, c, rows):
            copy.wait_send()
        if not last:
            pl.semaphore_signal(free_sem.at[d], inc=1, device_id={"expert": sibling},
                                device_id_type=MESH)

    def matches(target, meta):
        hit = jnp.zeros(target.shape, F32)
        gate = jnp.zeros(target.shape, F32)
        for k in range(8):
            same = target == meta[k : k + 1, :]
            hit = jnp.where(same, 1.0, hit)
            gate = jnp.where(same, meta[8 + k : 9 + k, :], gate)
        return hit.astype(jnp.bfloat16), jnp.sum(gate, axis=1, keepdims=True)

    def window_of(c, cc, lanes):
        start = CORES * CAP * c
        base = start // 16
        row = lax.broadcasted_iota(jnp.int32, (LOCAL * WINDOW, lanes), 0)
        expert = row // WINDOW
        rank = row % WINDOW - (start + CAP * cc - base * 16)
        return pl.multiple_of(base * 16, 16), expert, rank, (rank >= 0) & (rank < CAP)

    def place(first_row, pick, src, gate):
        def columns(n, carry):
            at = pl.ds(pl.multiple_of(n * COLS, COLS), COLS)
            got = jnp.dot(pick, src[:, at], preferred_element_type=F32)
            if gate is not None:
                got = got * gate
            got = got.astype(jnp.bfloat16)
            for e in range(LOCAL):
                there = (e, pl.ds(first_row, WINDOW), at)
                rows_out[there] = rows_out[there] + got[e * WINDOW : (e + 1) * WINDOW]
            return carry

        lax.fori_loop(0, width // COLS, columns, 0)

    def use_full(c, cc, src, meta_ref):
        first_row, expert, rank, ok = window_of(c, cc, tok)
        target = jnp.where(ok, (LOCAL * me + expert) * CAP + rank, -1).astype(F32)
        pick, gate = matches(target, meta_ref[...])
        place(first_row, pick, src, gate)

    def use_tail(c, cc, src, far, rows):
        first_row, expert, rank, ok = window_of(c, cc, rows)
        target = jnp.where(ok, CHIP_SLOTS * far + (LOCAL * core + expert) * CAP + rank, -1)
        lane = lax.broadcasted_iota(jnp.int32, target.shape, 1)
        pick = jnp.where(target == lane, 1.0, 0.0).astype(jnp.bfloat16)
        place(first_row, pick, src.at[pl.ds(0, rows)], None)

    def cut_down(d, c, ref):
        row = lax.broadcasted_iota(jnp.int32, (TAIL[-1], tok), 0)
        target = jnp.full(row.shape, -1, jnp.int32)
        for q in range(3):
            chip = chip_at(dirs[d] * (3 - q))
            inside = (row >= q * CHIP_SLOTS) & (row < (q + 1) * CHIP_SLOTS)
            target = jnp.where(inside, chip * CHIP_SLOTS + row - q * CHIP_SLOTS, target)
        pick, gate = matches(target.astype(F32), metas[c])

        def columns(n, carry):
            at = pl.ds(pl.multiple_of(n * COLS, COLS), COLS)
            got = jnp.dot(pick, blocks[c, :, at], preferred_element_type=F32) * gate
            ref[:, at] = got.astype(jnp.bfloat16)
            return carry

        lax.fori_loop(0, width // COLS, columns, 0)

    load_tokens.wait()
    for k in range(PIECES):
        for d in range(2):
            full(d, 1, k).start()

    load_weight.wait()
    logits = jnp.zeros((tok, experts), F32)
    for n in range(0, width, COLS):
        logits += jnp.dot(blocks[z, :, n : n + COLS], weight[n : n + COLS, :],
                          preferred_element_type=F32)
    raised = jnp.exp(logits - jnp.max(logits, axis=1, keepdims=True))
    probability = raised / jnp.sum(raised, axis=1, keepdims=True)
    mass = jnp.sum(probability, axis=0, keepdims=True)
    by_expert = logits.T
    ids = ids_ref[...]
    expert_row = lax.broadcasted_iota(jnp.int32, (experts, tok), 0)
    token_lane = lax.broadcasted_iota(jnp.int32, (experts, tok), 1)
    named = jnp.zeros((experts, tok), F32)
    for k in range(8):
        named = jnp.where(expert_row == ids[k : k + 1, :], 1.0, named)
    named16 = named.astype(jnp.bfloat16)
    earlier = (lax.broadcasted_iota(jnp.int32, (tok, tok), 0)
               < lax.broadcasted_iota(jnp.int32, (tok, tok), 1))
    before = jnp.dot(named16, jnp.where(earlier, 1.0, 0.0).astype(jnp.bfloat16),
                     preferred_element_type=F32)
    load = lax.dot_general(jnp.ones((8, tok), jnp.bfloat16), named16,
                           (((1,), (1,)), ((), ())), preferred_element_type=F32)[0:1]
    slots = []
    chosen = []
    for k in range(8):
        same = expert_row == ids[k : k + 1, :]
        rank = jnp.sum(jnp.where(same, before, 0.0), axis=0, keepdims=True)
        slots.append(ids[k : k + 1, :].astype(F32) * CAP + rank)
        chosen.append(jnp.sum(jnp.where(same, by_expert, 0.0), axis=0, keepdims=True))
    chosen = jnp.concatenate(chosen, axis=0)
    lifted = jnp.exp(chosen - jnp.max(chosen, axis=0, keepdims=True))
    gates = lifted / jnp.sum(lifted, axis=0, keepdims=True)
    metas[z, 0:8, :] = jnp.concatenate(slots, axis=0)
    metas[z, 8:16, :] = gates
    which = lax.broadcasted_iota(jnp.int32, (8, experts), 0)
    metas[z, 16:24, :] = jnp.where(which == 0, load, jnp.where(which == 1, mass, 0.0))

    for n in range(0, rows_out.shape[1], WINDOW):
        for e in range(LOCAL):
            rows_out[e, n : n + WINDOW, :] = jnp.zeros((WINDOW, width), jnp.bfloat16)

    for d in range(2):
        full(d, 1, META).start()
    pass_on(0, z, tok, True)
    use_full(z, core, blocks.at[z], metas.at[z])
    take_pass(0, z, tok)
    use_full(z, 1 - core, other.at[0], other_meta.at[0])
    end_pass(0, z, tok, False)

    def is_full(d, s):
        return s <= fars[d] - 3

    def tail_parts(d, s):
        return fars[d] - s + 1

    def arrive(d, s, k):
        (full if is_full(d, s) else tail)(d, s, k).wait_recv()

    def settle(d, s, k, static):
        if static and (s < 1 or s > fars[d]):
            return
        if static and not is_full(d, s) and k != META and k >= tail_parts(d, s):
            return
        (full if not static or is_full(d, s) or k == META else tail)(d, s, k).wait_send()

    TAIL_AT = {TAIL[n]: n - 1 for n in (1, 2, 3)}

    def handle(ways, s):
        for d, rows, first, last in ways:
            c = source(d, s)
            if rows == tok:
                use_full(c, core, blocks.at[c], metas.at[c])
            else:
                use_tail(c, core, blocks.at[c], TAIL_AT[rows], rows)
        for d, rows, first, last in ways:
            c = chip_at(dirs[d] * s)
            take_pass(d, c, rows)
            if rows == tok:
                use_full(c, 1 - core, other.at[d], other_meta.at[d])
            else:
                use_tail(c, 1 - core, other.at[d], TAIL_AT[rows], rows)
            end_pass(d, c, rows, last)

    def both_full(s, carry):
        for k in range(PIECES + 1):
            for d in range(2):
                full(d, s, k).wait_recv()
                full(d, s, k).wait_send()
                full(d, s + 1, k).start()
        for d in range(2):
            pass_on(d, source(d, s), tok, False)
        handle([(d, tok, False, False) for d in range(2)], s)
        return carry

    pl.semaphore_signal(free_sem.at[1], inc=1, device_id={"expert": sibling}, device_id_type=MESH)
    lax.fori_loop(1, far_short - 3, both_full, 0)

    for s in range(far_short - 3, far_long + 1):
        ways = []
        for d in range(2):
            if s > fars[d]:
                continue
            rows = tok if is_full(d, s) else TAIL[tail_parts(d, s)]
            ways.append((d, rows, False, s == fars[d]))
        for k in range(PIECES + 1):
            for d, rows, first, last in ways:
                if k == META or is_full(d, s) or k < tail_parts(d, s):
                    (full if k == META or is_full(d, s) else tail)(d, s, k).wait_recv()
                    settle(d, s, k, True)
                    if s < fars[d] and (k == META or is_full(d, s + 1)):
                        full(d, s + 1, k).start()
                    elif s < fars[d] and not is_full(d, s) and k < tail_parts(d, s + 1):
                        tail(d, s + 1, k).start()
        for d, rows, first, last in ways:
            if s == fars[d] - 3:
                ref = tail_short if d else tail_long
                cut_down(d, source(d, s), ref)
                for k in range(3):
                    tail(d, s + 1, k, ref).start()
        for d, rows, first, last in ways:
            pass_on(d, source(d, s), rows, False)
        handle(ways, s)

    total = metas[0, 16:24, :]
    for c in range(1, chips):
        total = total + metas[c, 16:24, :]
    sums[...] = total
    swap = pltpu.make_async_remote_copy(
        src_ref=sums, dst_ref=other_sums, send_sem=sum_sems.at[0], recv_sem=sum_sems.at[1],
        device_id={"expert": sibling}, device_id_type=MESH,
    )
    swap.start()
    write = pltpu.make_async_copy(rows_out, out_hbm, local_sem.at[0])
    write.start()
    swap.wait()
    both = sums[...] + other_sums[...]
    tokens_all = F32(tok * chips * CORES)
    summed = jnp.sum(both[0:1] * both[1:2])
    loss_ref[0] = experts * summed / (tokens_all * tokens_all * 8)
    write.wait()


def on_device(tokens, router_weight, expert_ids):
    tok, width = tokens.shape
    experts = router_weight.shape[1]
    devices = lax.axis_size("expert")
    chips = devices // CORES
    bf16 = jnp.bfloat16
    dma = pltpu.SemaphoreType.DMA
    return pl.pallas_call(
        kernel,
        name="dispatch",
        out_shape=(
            jax.ShapeDtypeStruct((LOCAL, devices * CAP, width), bf16),
            jax.ShapeDtypeStruct((1,), F32),
        ),
        in_specs=[
            pl.BlockSpec(memory_space=pltpu.VMEM),
            pl.BlockSpec(memory_space=pl.ANY),
            pl.BlockSpec(memory_space=pl.ANY),
        ],
        out_specs=(
            pl.BlockSpec(memory_space=pl.ANY),
            pl.BlockSpec(memory_space=pltpu.SMEM),
        ),
        scratch_shapes=[
            pltpu.VMEM((chips, tok, width), bf16),
            pltpu.VMEM((TAIL[-1], width), bf16),
            pltpu.VMEM((TAIL[-1], width), bf16),
            pltpu.VMEM((2, tok, width), bf16),
            pltpu.VMEM((chips, 24, tok), F32),
            pltpu.VMEM((2, 24, tok), F32),
            pltpu.VMEM((width, experts), bf16),
            pltpu.VMEM((LOCAL, devices * CAP, width), bf16),
            pltpu.VMEM((8, experts), F32),
            pltpu.VMEM((8, experts), F32),
            dma((2,)),
            dma((2, 2, PIECES + 1)),
            dma((2, chips // 2, PIECES + 1)),
            dma((2, 2)),
            dma((2, 2)),
            pltpu.SemaphoreType.REGULAR((2,)),
            dma((2,)),
        ],
        compiler_params=pltpu.CompilerParams(
            collective_id=0, has_side_effects=True, vmem_limit_bytes=60 * 1024 * 1024
        ),
    )(expert_ids.T, tokens, router_weight)


def solution(mesh):
    both = ("groups", "expert")
    return jax.shard_map(
        on_device, mesh=mesh, in_specs=(P(both, None), P(), P(both, None)),
        out_specs=(P("expert", "groups", None), P("groups")), check_vma=False,
    )
```

time: 1060 us -> 375 us (0.35)
  blocking collectives: 507 us -> 0 us
  Pallas kernels: 0 us -> 363 us
  waiting for transfers between devices: 349 us -> 0 us
  local copies, waits for them, and re-layouts: 100 us -> 8.8 us
  starting transfers between devices: 51.4 us -> 0 us
  other arithmetic: 45.9 us -> 0 us
    psum x2 -> x0, blocking collectives: 507 us -> none  [one_axis_at_a_time(): return functools.reduce(lax.psum, axes, shard)]
    pallas_call x0 -> x1, Pallas kernels: none -> 363 us  [on_device(): pl.pallas_call(kernel, name='dispatch', out_shape=(jax.ShapeDtypeStruct((...]
    all_to_all x2 -> x0, waiting for transfers between devices: 349 us -> none  [exchange_in_pieces(): lax.all_to_all(section, axis, split_axis=0, concat_axis=0, tiled=True)]
    all_to_all x2 -> x0, starting transfers between devices: 51.4 us -> none  [exchange_in_pieces(): lax.all_to_all(section, axis, split_axis=0, concat_axis=0, tiled=True)]
    split x3 -> x0, local copies, waits for them, and re-layouts: 27.7 us -> none  [exchange_in_pieces(): jnp.split(blocks, cut_rows(blocks.shape[split_at], pieces), axis=split_at)]
    concatenate x1 -> x0, other arithmetic: 25.9 us -> none  [exchange_in_pieces(): return in_order(jnp.concatenate(outs, axis=split_at), concat_dim)]
    gather x9 -> x0, local copies, waits for them, and re-layouts: 22.2 us -> none  [the longest x1 7.9 us: on_device(): picked = tokens[slot_token]]
    convert_element_type x2 -> x0, other arithmetic: 18 us -> none  [the longest x1 18 us: on_device(): (slot_gate[:, None] * picked.astype(jnp.float32)).astype(jnp.bfloat16)]
  transfers between devices with their start and end apart: 2 -> 0, of which waited for: 1 -> 0; matrix products, arithmetic and copies ran while one was open for 3% -> 0% of each run, Pallas kernels for 0% -> 0%
where the time goes in v1:
time: 375 us; the launch traced here: 374 us
  Pallas kernels  363 us (97%)
  local copies, waits for them, and re-layouts  8.8 us (2%)
    pallas_call x1, Pallas kernels, on_device(): pl.pallas_call(kernel, name='dispatch', out_shape=(jax.ShapeDtypeStruct((...  363 us
    unnamed x1, local copies, waits for them, and re-layouts  8.8 us

profile of v1, /device:TPU:37, one launch (start us, length us, event | category | flops | bytes accessed | tf_op | source)
XLA Modules:
  0.0 374.4 jit_solution(7976727604191682686)
XLA Ops:
  0.6 363.1 %dispatch.1 = (bf16[2,576,4096]{2,1,0:T(8,128)(2,1)}, f32[1]{0:T(128)}) custom-call(s32[8,128]{1,0:T(8,128)} %bitcast.1, bf16[128,4096]{1,0:T(8,128)(2,1)} %tokens_hbm.1, bf16[4096,128]{1,0:T(8,128)(2,1)} %weight_hbm.1), custom_call_target="tpu_custom_call" | custom-call | tf_op jit(solution)/shard_map/dispatch/pallas_call | solution.py:325
  363.8 8.8 %copy.7 = bf16[2,576,4096]{2,1,0:T(8,128)(2,1)} copy(bf16[2,576,4096]{2,1,0:T(8,128)(2,1)} %get-tuple-element.4) | data formatting | bytes 18874368
